TPU v7x, 256 devices: a whole 4x4x8 slice. The times are simulated.
256 devices in a mesh: gx: 8 (over y, x_hi), gy: 4 (over x_lo, core), gz: 8 (over z).
Axes of the slice: x: 4 (x_hi: 2, x_lo: 2; x = x_hi * 2 + x_lo), y: 4, z: 8, core: 2. Of those that a mesh axis runs over, the one named last changes fastest.
Arguments:
- source: bfloat16 [512, 512, 512], P('gz', 'gx', 'gy'), may hold values from -6 to 6
- forward_x: bfloat16 [512, 512], replicated, may hold values from -0.25 to 0.25
- forward_y: bfloat16 [512, 512], replicated, may hold values from -0.25 to 0.25
- forward_z: bfloat16 [512, 512], replicated, may hold values from -0.25 to 0.25
- inverse_x: bfloat16 [512, 512], replicated, may hold values from -0.25 to 0.25
- inverse_y: bfloat16 [512, 512], replicated, may hold values from -0.25 to 0.25
- inverse_z: bfloat16 [512, 512], replicated, may hold values from -0.25 to 0.25
- values_x: float32 [512], replicated, may hold values from 0.1 to 2
- values_y: float32 [512], replicated, may hold values from 0.1 to 2
- values_z: float32 [512], replicated, may hold values from 0.1 to 2
Outputs:
- solution: bfloat16 [512, 512, 512], P('gz', 'gx', 'gy')
All inputs are finite; a program needn't handle non-finite values.
Results may differ from a plain program's by a relative error of at most 0.015.
Values may be sent and summed in bfloat16 or wider, within the bound.
A program may use at most 64 MiB of HBM per device.

v0:
```python
import jax
import jax.numpy as jnp
from jax import lax
from jax.sharding import PartitionSpec as P


def cut_along(shard, dim, length):
    shape = shard.shape
    pieces = shard.reshape(*shape[:dim], length, shape[dim] // length, *shape[dim + 1 :])
    return jnp.moveaxis(pieces, dim, 0)


def laid_out(pieces, dim):
    shape = list(pieces.shape[1:])
    shape[dim] *= pieces.shape[0]
    return jnp.moveaxis(pieces, 0, dim).reshape(shape)


def one_exchange(shard, axis, axes, splits, concats):
    sizes = [lax.axis_size(a) for a in axes]
    pieces = cut_along(shard, splits[0], sizes[0])
    pieces = jnp.moveaxis(cut_along(pieces, splits[1] + 1, sizes[1]), 0, 1)
    inside = pieces.shape[2:]
    pieces = pieces.reshape(-1, *inside)
    pieces = lax.all_to_all(pieces, axis, split_axis=0, concat_axis=0, tiled=True)
    pieces = laid_out(pieces.reshape(*sizes, *inside), concats[0] + 1)
    return laid_out(pieces, concats[1])


def along_last(data, basis):
    shape = data.shape
    flat = data.reshape(-1, shape[-1])
    out = lax.dot_general(flat, basis, (((1,), (1,)), ((), ())), preferred_element_type=jnp.float32)
    return out.astype(jnp.bfloat16).reshape(shape[:-1] + (basis.shape[0],))


def along_middle(data, basis):
    out = jnp.einsum("qn,anb->aqb", basis, data, preferred_element_type=jnp.float32)
    return out.astype(jnp.bfloat16)


def along_first(data, basis):
    depth, rows, cols = data.shape
    out = jnp.dot(basis, data.reshape(depth, rows * cols), preferred_element_type=jnp.float32)
    return out.astype(jnp.bfloat16).reshape(basis.shape[0], rows, cols)


def to_plane(block):
    count_y = lax.axis_size("gx")
    count_x = lax.axis_size("gy")
    depth, rows, cols = block.shape
    five = block.reshape(count_y, count_x, depth // (count_x * count_y), rows, cols)
    moved = one_exchange(five, ("gx", "gy"), ("gx", "gy"), (0, 1), (3, 4))
    return moved.reshape(depth // (count_x * count_y), rows * count_y, cols * count_x)


def from_plane(plane):
    count_y = lax.axis_size("gx")
    count_x = lax.axis_size("gy")
    depth, rows, cols = plane.shape
    five = plane.reshape(1, 1, depth, rows, cols)
    moved = one_exchange(five, ("gx", "gy"), ("gx", "gy"), (3, 4), (0, 1))
    return moved.reshape(count_y * count_x * depth, rows // count_y, cols // count_x)


def divide(data, values_z, values_y, values_x, y_start, x_start):
    depth, rows, cols = data.shape
    lam_y = lax.dynamic_slice_in_dim(values_y, y_start, rows)
    lam_x = lax.dynamic_slice_in_dim(values_x, x_start, cols)
    denom = values_z[:, None, None] + lam_y[None, :, None] + lam_x[None, None, :]
    return (data.astype(jnp.float32) / denom).astype(jnp.bfloat16)


def plane_depth(plane, forward_z, inverse_z, values_z, values_y, values_x):
    count_y = lax.axis_size("gx")
    count_x = lax.axis_size("gy")
    count_z = lax.axis_size("gz")
    thick, full_y, full_x = plane.shape
    total_z = forward_z.shape[0]
    gathered = lax.all_to_all(plane, "gz", split_axis=1, concat_axis=0, tiled=True)
    stacked = gathered.reshape(1, 1, count_z * thick, full_y // count_z, full_x)
    spread = one_exchange(stacked, ("gx", "gy"), ("gx", "gy"), (3, 4), (0, 1))
    slim_y = full_y // (count_z * count_y)
    slim_x = full_x // count_x
    lines = spread.reshape(total_z, slim_y, slim_x)
    mixed_fwd = forward_z.reshape(total_z, count_z, count_y, count_x, thick)
    mixed_fwd = mixed_fwd.transpose(0, 2, 3, 1, 4).reshape(total_z, total_z)
    mixed_inv = inverse_z.reshape(count_z, count_y, count_x, thick, total_z)
    mixed_inv = mixed_inv.transpose(1, 2, 0, 3, 4).reshape(total_z, total_z)
    step_c = along_first(lines, mixed_fwd)
    y_start = lax.axis_index("gz") * (full_y // count_z) + lax.axis_index("gx") * slim_y
    scaled = divide(step_c, values_z, values_y, values_x, y_start, lax.axis_index("gy") * slim_x)
    step_d = along_first(scaled, mixed_inv)
    five = step_d.reshape(count_y, count_x, count_z * thick, slim_y, slim_x)
    back = one_exchange(five, ("gx", "gy"), ("gx", "gy"), (0, 1), (3, 4))
    back = back.reshape(count_z * thick, full_y // count_z, full_x)
    return lax.all_to_all(back, "gz", split_axis=0, concat_axis=1, tiled=True)


def on_device(
    source,
    forward_x,
    forward_y,
    forward_z,
    inverse_x,
    inverse_y,
    inverse_z,
    values_x,
    values_y,
    values_z,
):
    plane = along_middle(along_last(to_plane(source), forward_x), forward_y)
    plane = plane_depth(plane, forward_z, inverse_z, values_z, values_y, values_x)
    return from_plane(along_last(along_middle(plane, inverse_y), inverse_x))


def solution(mesh):
    return jax.shard_map(
        on_device,
        mesh=mesh,
        in_specs=(P("gz", "gx", "gy"), P(), P(), P(), P(), P(), P(), P(), P(), P()),
        out_specs=P("gz", "gx", "gy"),
        check_vma=False,
    )
```

profile of v0, /device:TPU:1, one launch (start us, length us, event | category | flops | bytes accessed | tf_op | source)
XLA Modules:
  0.0 171.5 jit_solution(13837438035608125189)
XLA Ops:
  0.0 25.8 %all_to_all.53 = bf16[32,1,1,2,64,128]{5,4,3,2,1,0:T(8,128)(2,1)S(1)} all-to-all(bf16[32,1,1,2,64,128]{5,4,3,2,1,0:T(8,128)(2,1)} %bitcast.123), channel_id=1, replica_groups=mesh['gx'=8,'gy'=4,'gz'=8] {'gx','gy'}, dimensions={0} | all-to-all | bytes 2097152 | tf_op jit(solution)/shard_map/all_to_all | solution.py:25
  25.9 0.8 copy.57
  26.7 0.7 convolution_convert_fusion.5
  27.7 0.8 fusion.2
  28.5 1.0 copy.59
  29.5 35.9 %all_to_all.54 = bf16[2,512,512]{2,0,1:T(2,128)(2,1)S(1)} all-to-all(bf16[2,512,512]{2,0,1:T(2,128)(2,1)S(1)} %copy.59), channel_id=1, replica_groups=mesh['gx'=8,'gy'=4,'gz'=8] {'gz'}, dimensions={1} | all-to-all | bytes 2097152 | tf_op jit(solution)/shard_map/all_to_all | solution.py:80
  66.0 1.3 copy.62
  67.3 5.6 %all-to-all-start.2 = ((bf16[32,1,1,16,8,128]{5,4,3,2,1,0:T(8,128)(2,1)}), bf16[32,1,1,16,8,128]{5,4,3,2,1,0:T(8,128)(2,1)S(1)}, u32[]{:S(2)}, u32[]{:S(2)}) async-start(bf16[32,1,1,16,8,128]{5,4,3,2,1,0:T(8,128)(2,1)} %bitcast.14), calls=%async_computation.2 | async-start | bytes 2097152 | tf_op jit(solution)/shard_map/all_to_all | solution.py:25
  73.4 0.5 copy.65
  74.1 1.2 reshape.96
  75.4 0.5 copy.91
  76.2 0.8 dynamic_slice.6
  76.9 0.8 dynamic_slice.7
  77.7 12.2 %all-to-all-done.2 = bf16[32,1,1,16,8,128]{5,4,3,2,1,0:T(8,128)(2,1)S(1)} async-done(((bf16[32,1,1,16,8,128]{5,4,3,2,1,0:T(8,128)(2,1)}), bf16[32,1,1,16,8,128]{5,4,3,2,1,0:T(8,128)(2,1)S(1)}, u32[]{:S(2)}, u32[]{:S(2)}) %all-to-all-start.2) | async-done | bytes 1048608 | tf_op jit(solution)/shard_map/all_to_all | solution.py:25
  90.0 0.8 fusion.1
  90.8 0.7 fusion.3
  92.3 20.7 %all_to_all.55 = bf16[32,1,1,16,8,128]{5,4,3,2,1,0:T(8,128)(2,1)S(1)} all-to-all(bf16[32,1,1,16,8,128]{5,4,3,2,1,0:T(8,128)(2,1)S(1)} %bitcast.115), channel_id=1, replica_groups=mesh['gx'=8,'gy'=4,'gz'=8] {'gx','gy'}, dimensions={0} | all-to-all | bytes 2097152 | tf_op jit(solution)/shard_map/all_to_all | solution.py:25
  113.3 0.9 copy.70
  114.6 31.6 %all_to_all.56 = bf16[16,64,512]{2,1,0:T(8,128)(2,1)S(1)} all-to-all(bf16[16,64,512]{2,1,0:T(8,128)(2,1)S(1)} %reshape_reshape.10), channel_id=1, replica_groups=mesh['gx'=8,'gy'=4,'gz'=8] {'gz'}, dimensions={0} | all-to-all | bytes 2097152 | tf_op jit(solution)/shard_map/all_to_all | solution.py:97
  146.3 0.9 copy-done.4
  147.2 0.7 convolution_convert_fusion
  148.3 0.7 convolution_convert_fusion.1
  149.5 21.0 %all_to_all.57 = bf16[32,1,1,2,64,128]{5,4,3,2,1,0:T(8,128)(2,1)S(1)} all-to-all(bf16[32,1,1,2,64,128]{5,4,3,2,1,0:T(8,128)(2,1)S(1)} %bitcast.111), channel_id=1, replica_groups=mesh['gx'=8,'gy'=4,'gz'=8] {'gx','gy'}, dimensions={0} | all-to-all | bytes 2097152 | tf_op jit(solution)/shard_map/all_to_all | solution.py:25
  170.5 1.0 copy.93
  (30 shorter events, 4.4 us)
Async XLA Ops:
  0.0 26.7 %copy-start = (bf16[512,512]{1,0:T(8,128)(2,1)S(1)}, bf16[512,512]{1,0:T(8,128)(2,1)}, u32[]{:S(2)}) copy-start(bf16[512,512]{1,0:T(8,128)(2,1)} %param.11) | copy-start | bytes 1572868
  26.7 1.0 copy-start.3
  67.3 5.7 %copy-start.1 = (bf16[512,512]{1,0:T(8,128)(2,1)S(1)}, bf16[512,512]{1,0:T(8,128)(2,1)}, u32[]{:S(2)}) copy-start(bf16[512,512]{1,0:T(8,128)(2,1)} %param.13) | copy-start | bytes 1572868
  67.3 22.7 %all-to-all-start.2 = ((bf16[32,1,1,16,8,128]{5,4,3,2,1,0:T(8,128)(2,1)}), bf16[32,1,1,16,8,128]{5,4,3,2,1,0:T(8,128)(2,1)S(1)}, u32[]{:S(2)}, u32[]{:S(2)}) async-start(bf16[32,1,1,16,8,128]{5,4,3,2,1,0:T(8,128)(2,1)} %bitcast.14), calls=%async_computation.2 | async-start | bytes 2097152 | tf_op jit(solution)/shard_map/all_to_all | solution.py:25
  75.4 2.3 %copy-start.2 = (f32[512]{0:T(512)S(1)}, f32[512]{0:T(512)}, u32[]{:S(2)}) copy-start(f32[512]{0:T(512)} %param.19) | copy-start | bytes 6148
  146.2 1.0 copy-start.4
  147.2 1.0 copy-start.5
where the time goes:
time: 172 us
  blocking collectives  135 us (78%)
  local copies, waits for them, and re-layouts  13.8 us (8%)
  waiting for transfers between devices  12.2 us (7%)
  starting transfers between devices  5.64 us (3%)
  matrix products  4.43 us (3%)
    all_to_all x3, blocking collectives, one_exchange(): lax.all_to_all(pieces, axis, split_axis=0, concat_axis=0, tiled=True)  67.4 us
    all_to_all x1, blocking collectives, plane_depth(): lax.all_to_all(plane, 'gz', split_axis=1, concat_axis=0, tiled=True)  35.9 us
    all_to_all x1, blocking collectives, plane_depth(): return lax.all_to_all(back, 'gz', split_axis=0, concat_axis=1, tiled=True)  31.6 us
    all_to_all x1, waiting for transfers between devices, one_exchange(): lax.all_to_all(pieces, axis, split_axis=0, concat_axis=0, tiled=True)  12.2 us
    all_to_all x1, starting transfers between devices, one_exchange(): lax.all_to_all(pieces, axis, split_axis=0, concat_axis=0, tiled=True)  5.64 us
  transfers between devices with their start and end apart: 1, of which 1 were waited for; matrix products, arithmetic and copies ran while one was open for 3% of the time, Pallas kernels for 0%

commit v1 on v0

v1 whole, which is shorter than its diff:
```python
import functools

import jax
import jax.numpy as jnp
from jax import lax
from jax.experimental import pallas as pl
from jax.experimental.pallas import tpu as pltpu
from jax.sharding import PartitionSpec as P

MESH = pl.DeviceIdType.MESH
F32 = jnp.float32
BF16 = jnp.bfloat16
NX, NY, NZ = 8, 4, 8
N = 512
K = 4
PITCH = N + 8
OPITCH = 128 + 8
FAR_FIRST = (4, 3, 5, 2, 6, 1, 7)


def dot(a, b):
    return jnp.dot(a, b, preferred_element_type=F32)


def dot_t(a, b):
    return lax.dot_general(a, b, (((1,), (1,)), ((), ())), preferred_element_type=F32)


def kernel(
    src, fx, fy, fz, ix, iy, iz, vx, vy, vz, out,
    xin, psend, ybuf, yout, zbuf, zlines, recip, scaled, olines, zsend, ybuf2, yout2, pbuf, xg, xout,
    weights, izp, vxs, vys, vzs, recv, send, wsem, vsem, lsem,
):
    gx, gy, gz = lax.axis_index("gx"), lax.axis_index("gy"), lax.axis_index("gz")
    me = gz * NY + gy

    def dev(a, b, c):
        return {"gx": a, "gy": b, "gz": c}

    def remote(s, d, stage, k, where):
        pltpu.make_async_remote_copy(
            src_ref=s, dst_ref=d, send_sem=send.at[stage], recv_sem=recv.at[stage, k],
            device_id=where, device_id_type=MESH,
        ).start()

    def arrived(ref, sem):
        pltpu.make_async_copy(ref, ref, sem).wait()

    barrier = pltpu.get_barrier_semaphore()
    for d in range(1, NX):
        pl.semaphore_signal(barrier, inc=1, device_id=dev(lax.rem(gx + d, NX), gy, gz), device_id_type=MESH)
    for c in range(NZ):
        for b in range(NY):
            if b or c:
                pl.semaphore_signal(
                    barrier, inc=1, device_id=dev(gx, lax.rem(gy + b, NY), lax.rem(gz + c, NZ)), device_id_type=MESH
                )

    for k in range(K):
        pltpu.make_async_copy(
            src.at[pl.ds(16 * gy + 4 * k, 4)],
            xin.at[k, :, :, pl.ds(pl.multiple_of(128 * gy, 128), 128)],
            recv.at[0, k],
        ).start()
    loads = [pltpu.make_async_copy(w, weights.at[i], wsem.at[i]) for i, w in enumerate((fx, fy, fz, iz, iy, ix))]
    for c in loads:
        c.start()
    vloads = [pltpu.make_async_copy(v, s, vsem.at[i]) for i, (v, s) in enumerate(((vx, vxs), (vy, vys), (vz, vzs)))]
    for c in vloads:
        c.start()

    pl.semaphore_wait(barrier, NX - 1 + NZ * NY - 1)

    for k in range(K):
        for d in range(1, NY):
            to = lax.rem(gy + d, NY)
            remote(
                src.at[pl.ds(16 * to + 4 * k, 4)],
                xin.at[k, :, :, pl.ds(pl.multiple_of(128 * gy, 128), 128)],
                0, k, dev(gx, to, gz),
            )

    lane = lax.broadcasted_iota(jnp.int32, (8, 128), 1)
    sub = lax.broadcasted_iota(jnp.int32, (8, 128), 0)
    low = lane < 64

    def exchange_halves(a, b):
        keep = jnp.broadcast_to(lax.broadcasted_iota(jnp.int32, (1, 128), 1) < 64, a.shape)
        return (
            jnp.where(keep, a, pltpu.roll(b, 64, 1)),
            jnp.where(keep, pltpu.roll(a, 64, 1), b),
        )

    for c in vloads:
        c.wait()
    along_p = jnp.zeros((8, 128), F32)
    for i in range(64):
        along_p = jnp.where((lane & 63) == i, vxs[64 * gx + i], along_p)
    along_qp = [
        along_p + jnp.where(low, vys[16 * me + q], vys[16 * me + q + 8]) for q in range(8)
    ]

    def reciprocals(g, _):
        col = jnp.zeros((8, 128), F32)
        for i in range(8):
            col = jnp.where(sub == i, vzs[8 * g + i], col)
        rows = pl.ds(pl.multiple_of(8 * g, 8), 8)
        for q in range(8):
            recip[rows, 128 * q : 128 * (q + 1)] = 1.0 / (col + along_qp[q])
        return 0

    lax.fori_loop(0, N // 8, reciprocals, 0)

    loads[3].wait()
    row = lax.broadcasted_iota(jnp.int32, (N, N), 0)
    wanted = ((row & 127) >> 2) * 16 + (row >> 7) * 4 + (row & 3)
    order = (lax.broadcasted_iota(jnp.int32, (N, N), 1) == wanted).astype(F32).astype(BF16)
    izp[...] = dot(order, weights[3]).astype(BF16)

    def forward_x(k):
        arrived(xin.at[k], recv.at[0, k])
        o = dot_t(xin[k].reshape(256, N), weights[0]).reshape(2, 2, 64, N)
        for zp in range(2):
            for t in range(4):
                a, b = exchange_halves(o[zp, 0, :, 128 * t : 128 * (t + 1)], o[zp, 1, :, 128 * t : 128 * (t + 1)])
                psend[k, 2 * t, zp] = a.astype(BF16)
                psend[k, 2 * t + 1, zp] = b.astype(BF16)
        rows = pl.ds(pl.multiple_of(64 * gx, 64), 64)
        for d in range(1, NX):
            to = lax.rem(gx + d, NX)
            remote(psend.at[k, to], ybuf.at[k, :, rows, :], 1, k, dev(to, gy, gz))
        for zp in range(2):
            ybuf[k, zp, rows, :] = psend[k, gx, zp]

    def forward_y(k):
        arrived(psend.at[k, 0:7], recv.at[1, k])
        o = dot(weights[1], jnp.concatenate([ybuf[k, 0], ybuf[k, 1]], axis=1))
        for zp in range(2):
            yout[k, zp] = o[:, 128 * zp : 128 * (zp + 1)].astype(BF16)

        def to_lines(b, c):
            to_b, to_c = lax.rem(gy + b, NY), lax.rem(gz + c, NZ)
            rows = pl.ds(pl.multiple_of(16 * (to_c * NY + to_b), 16), 16)
            remote(yout.at[k, :, rows, :], zbuf.at[k, me], 2, k, dev(gx, to_b, to_c))

        for c in FAR_FIRST:
            lax.fori_loop(0, NY, lambda b, _, c=c: (to_lines(b, c), 0)[1], 0)
        lax.fori_loop(1, NY, lambda b, _: (to_lines(b, 0), 0)[1], 0)
        rows = pl.ds(pl.multiple_of(16 * me, 16), 16)
        for zp in range(2):
            zbuf[k, me, zp] = yout[k, zp, rows, :]

    def to_z_rows(k):
        arrived(zbuf.at[k, 0:31], recv.at[2, k])

        def some(g, _):
            for s in range(8):
                for zp in range(2):
                    tile = zbuf[k, 8 * g + s, zp].astype(F32)
                    a, b = exchange_halves(tile[:8], tile[8:])
                    z = 16 * (8 * g + s) + 4 * k + 2 * zp
                    zlines[pl.ds(z, 8, stride=PITCH), :] = a
                    zlines[pl.ds(z + 1, 8, stride=PITCH), :] = b
            return 0

        lax.fori_loop(0, 4, some, 0)

    def along_z():
        for h in range(4):
            d = jnp.concatenate(
                [zlines[PITCH * q : PITCH * q + N, :] for q in (2 * h, 2 * h + 1)], axis=1
            ).astype(BF16)
            c = dot(weights[2], d).astype(BF16).astype(F32)
            scaled[:, 256 * h : 256 * (h + 1)] = (c * recip[:, 256 * h : 256 * (h + 1)]).astype(BF16)

    def from_z_rows(k):
        for h in range(4):
            o = dot(izp[128 * k : 128 * (k + 1), :], scaled[:, 256 * h : 256 * (h + 1)])
            for j in range(2):
                q = 2 * h + j
                olines[k, OPITCH * q : OPITCH * q + 128, :] = o[:, 128 * j : 128 * (j + 1)]

        def some(g, _):
            for s in range(8):
                for zp in range(2):
                    at = 4 * (8 * g + s) + 2 * zp
                    a, b = exchange_halves(
                        olines[k, pl.ds(at, 8, stride=OPITCH), :], olines[k, pl.ds(at + 1, 8, stride=OPITCH), :]
                    )
                    zsend[k, 8 * g + s, zp] = jnp.concatenate([a, b], axis=0).astype(BF16)
            return 0

        lax.fori_loop(0, 4, some, 0)
        rows = pl.ds(pl.multiple_of(16 * me, 16), 16)

        def to_planes(b, c):
            to_b, to_c = lax.rem(gy + b, NY), lax.rem(gz + c, NZ)
            remote(zsend.at[k, to_c * NY + to_b], ybuf2.at[k, :, rows, :], 3, k, dev(gx, to_b, to_c))

        for c in FAR_FIRST:
            lax.fori_loop(0, NY, lambda b, _, c=c: (to_planes(b, c), 0)[1], 0)
        lax.fori_loop(1, NY, lambda b, _: (to_planes(b, 0), 0)[1], 0)
        for zp in range(2):
            ybuf2[k, zp, rows, :] = zsend[k, me, zp]

    def inverse_y(k):
        arrived(zsend.at[k, 0:31], recv.at[3, k])
        o = dot(weights[4], jnp.concatenate([ybuf2[k, 0], ybuf2[k, 1]], axis=1))
        for zp in range(2):
            yout2[k, zp] = o[:, 128 * zp : 128 * (zp + 1)].astype(BF16)
        for d in range(1, NX):
            to = lax.rem(gx + d, NX)
            rows = pl.ds(pl.multiple_of(64 * to, 64), 64)
            remote(yout2.at[k, :, rows, :], pbuf.at[k, gx], 4, k, dev(to, gy, gz))
        rows = pl.ds(pl.multiple_of(64 * gx, 64), 64)
        for zp in range(2):
            pbuf[k, gx, zp] = yout2[k, zp, rows, :]

    def inverse_x(k):
        arrived(pbuf.at[k, 0:7], recv.at[4, k])
        for zp in range(2):
            for t in range(4):
                a, b = exchange_halves(pbuf[k, 2 * t, zp].astype(F32), pbuf[k, 2 * t + 1, zp].astype(F32))
                xg[k, 2 * zp, :, 128 * t : 128 * (t + 1)] = a.astype(BF16)
                xg[k, 2 * zp + 1, :, 128 * t : 128 * (t + 1)] = b.astype(BF16)
        o = dot_t(xg[k].reshape(256, N), weights[5])
        xout[k] = o.astype(BF16).reshape(4, 64, N)
        slab = pl.ds(16 * gy + 4 * k, 4)
        for d in range(1, NY):
            to = lax.rem(gy + d, NY)
            columns = pl.ds(pl.multiple_of(128 * to, 128), 128)
            remote(xout.at[k, :, :, columns], out.at[slab], 5, 0, dev(gx, to, gz))
        columns = pl.ds(pl.multiple_of(128 * gy, 128), 128)
        pltpu.make_async_copy(xout.at[k, :, :, columns], out.at[slab], lsem).start()

    loads[0].wait()
    forward_x(0)
    loads[1].wait()
    forward_x(1)
    forward_y(0)
    forward_x(2)
    forward_y(1)
    forward_x(3)
    forward_y(2)
    forward_y(3)
    for k in range(K):
        to_z_rows(k)
    loads[2].wait()
    along_z()
    for k in range(K):
        from_z_rows(k)
    loads[4].wait()
    loads[5].wait()
    inverse_y(0)
    for k in range(1, K):
        inverse_y(k)
        inverse_x(k - 1)
    inverse_x(K - 1)

    arrived(out.at[0:48], recv.at[5, 0])
    arrived(out.at[0:16], lsem)
    arrived(out.at[0:48], send.at[0])
    arrived(out.at[0:48], send.at[5])
    arrived(psend.at[:, 0:7], send.at[1])
    arrived(psend.at[:, 0:7], send.at[4])
    arrived(zbuf.at[:, 0:31], send.at[2])
    arrived(zbuf.at[:, 0:31], send.at[3])


def on_device(source, *rest):
    pieces = pltpu.VMEM((K, NX, 2, 64, 128), BF16)
    planes = pltpu.VMEM((K, 2, N, 128), BF16)
    lines = pltpu.VMEM((K, NZ * NY, 2, 16, 128), BF16)
    rows = pltpu.VMEM((K, 4, 64, N), BF16)
    return pl.pallas_call(
        kernel,
        out_shape=jax.ShapeDtypeStruct(source.shape, BF16),
        in_specs=[pl.BlockSpec(memory_space=pl.ANY)] * 10,
        out_specs=pl.BlockSpec(memory_space=pl.ANY),
        scratch_shapes=[
            rows,
            pieces,
            planes,
            planes,
            lines,
            pltpu.VMEM((8 * PITCH, 128), F32),
            pltpu.VMEM((N, 1024), F32),
            pltpu.VMEM((N, 1024), BF16),
            pltpu.VMEM((K, 8 * OPITCH, 128), F32),
            lines,
            planes,
            planes,
            pieces,
            rows,
            rows,
            pltpu.VMEM((6, N, N), BF16),
            pltpu.VMEM((N, N), BF16),
            pltpu.SMEM((N,), F32),
            pltpu.SMEM((N,), F32),
            pltpu.SMEM((N,), F32),
            pltpu.SemaphoreType.DMA((6, K)),
            pltpu.SemaphoreType.DMA((6,)),
            pltpu.SemaphoreType.DMA((6,)),
            pltpu.SemaphoreType.DMA((3,)),
            pltpu.SemaphoreType.DMA,
        ],
        compiler_params=pltpu.CompilerParams(
            collective_id=0, has_side_effects=True, vmem_limit_bytes=60 * 1024 * 1024
        ),
    )(source, *rest)


def solution(mesh):
    return jax.shard_map(
        on_device,
        mesh=mesh,
        in_specs=(P("gz", "gx", "gy"),) + (P(),) * 9,
        out_specs=P("gz", "gx", "gy"),
        check_vma=False,
    )
```

time: 172 us -> 98.8 us (0.57)
  blocking collectives: 135 us -> 0 us
  Pallas kernels: 0 us -> 96.4 us
  waiting for transfers between devices: 12.2 us -> 0 us
  local copies, waits for them, and re-layouts: 13.8 us -> 2.26 us
  starting transfers between devices: 5.64 us -> 0 us
  matrix products: 4.43 us -> 0 us
    all_to_all x5 -> x0, blocking collectives: 135 us -> none  [the longest x3 67.4 us: one_exchange(): lax.all_to_all(pieces, axis, split_axis=0, concat_axis=0, tiled=True)]
    pallas_call x0 -> x1, Pallas kernels: none -> 96.4 us  [on_device(): pl.pallas_call(kernel, out_shape=jax.ShapeDtypeStruct(source.shape, BF16)...]
    all_to_all x1 -> x0, waiting for transfers between devices: 12.2 us -> none  [one_exchange(): lax.all_to_all(pieces, axis, split_axis=0, concat_axis=0, tiled=True)]
    all_to_all x1 -> x0, starting transfers between devices: 5.64 us -> none  [one_exchange(): lax.all_to_all(pieces, axis, split_axis=0, concat_axis=0, tiled=True)]
    dot_general x6 -> x0, matrix products: 4.43 us -> none  [the longest x2 1.49 us: along_first(): jnp.dot(basis, data.reshape(depth, rows * cols), preferred_element_type=j...]
    transpose x5 -> x0, local copies, waits for them, and re-layouts: 2.61 us -> none  [the longest x4 2.07 us: laid_out(): return jnp.moveaxis(pieces, 0, dim).reshape(shape)]
    reshape x5 -> x0, local copies, waits for them, and re-layouts: 2.38 us -> none  [the longest x2 1.78 us: plane_depth(): mixed_inv = inverse_z.reshape(count_z, count_y, count_x, thick, total_z)]
  transfers between devices with their start and end apart: 1 -> 0, of which waited for: 1 -> 0; matrix products, arithmetic and copies ran while one was open for 3% -> 0% of each run, Pallas kernels for 0% -> 0%
where the time goes in v1:
time: 98.8 us; the launch traced here: 98.7 us
  Pallas kernels  96.4 us (98%)
  local copies, waits for them, and re-layouts  2.26 us (2%)
    pallas_call x1, Pallas kernels, on_device(): pl.pallas_call(kernel, out_shape=jax.ShapeDtypeStruct(source.shape, BF16)...  96.4 us
    unnamed x1, local copies, waits for them, and re-layouts  2.26 us

profile of v1, /device:TPU:1, one launch (start us, length us, event | category | flops | bytes accessed | tf_op | source)
XLA Modules:
  0.0 98.7 jit_solution(12781411886138535763)
XLA Ops:
  0.0 96.4 %shard_map.100 = bf16[64,64,128]{2,1,0:T(8,128)(2,1)} custom-call(bf16[64,64,128]{2,1,0:T(8,128)(2,1)} %src.1, bf16[512,512]{1,0:T(8,128)(2,1)} %fx.1, bf16[512,512]{1,0:T(8,128)(2,1)} %fy.1, bf16[512,512]{1,0:T(8,128)(2,1)} %fz.1, bf16[512,512]{1,0:T(8,128)(2,1)} %ix.1, bf16[512,512]{1,0:T(8,128)(2,1)} %iy.1, bf16[512,512]{1,0:T(8,128)(2,1)} %iz.1, f32[512]{0:T(512)} %vx.1, ...), custom_call_target="tpu_custom_call" | custom-call | tf_op jit(solution)/shard_map/pallas_call | solution.py:275
  96.4 2.3 %copy.12 = bf16[64,64,128]{2,1,0:T(8,128)(2,1)} copy(bf16[64,64,128]{2,1,0:T(8,128)(2,1)} %shard_map.100) | data formatting | bytes 2097152

commit v2 on v1

v2 whole, which is shorter than its diff:
```python
import jax
import jax.numpy as jnp
from jax import lax
from jax.experimental import pallas as pl
from jax.experimental.pallas import tpu as pltpu
from jax.sharding import PartitionSpec as P

MESH = pl.DeviceIdType.MESH
F32 = jnp.float32
BF16 = jnp.bfloat16
NX, NY, NZ = 8, 4, 8
N = 512
PAIRS = 8
FORWARD = ((0, 1), (1, 1), (2, 2), (4, 2), (6, 2))
INVERSE = ((0, 1), (1, 2), (3, 2), (5, 1), (6, 1), (7, 1))
FORWARD_ORDER = (
    ("x", 0), ("x", 1), ("x", 2), ("y", 0), ("z", 0, 0), ("z", 0, 1), ("y", 1), ("z", 1, 0), ("z", 1, 1),
    ("x", 3), ("y", 2), ("z", 2, 0), ("z", 2, 1), ("x", 4), ("y", 3), ("z", 3, 0), ("y", 4), ("z", 4, 0),
    ("z", 3, 1), ("z", 4, 1),
)
INVERSE_ORDER = (("y", 0), ("y", 1), ("x", 0), ("y", 2), ("x", 1), ("y", 3), ("x", 2), ("y", 4), ("x", 3), ("y", 5), ("x", 4), ("x", 5))
PITCH = N + 8
FAR_FIRST = (4, 3, 5, 2, 6, 1, 7)


def dot(a, b):
    return jnp.dot(a, b, preferred_element_type=F32)


def dot_t(a, b):
    return lax.dot_general(a, b, (((1,), (1,)), ((), ())), preferred_element_type=F32)


def kernel(
    src, fx, fy, fz, ix, iy, iz, vx, vy, vz, out,
    staged, xin, psend, ybuf, yout, zbuf, zlines, recip, scaled, olines, zsend, ybuf2, yout2, pbuf, xg, xout,
    weights, izp, vxs, vys, vzs, recv, send, wsem, vsem, ssem,
):
    gx, gy, gz = lax.axis_index("gx"), lax.axis_index("gy"), lax.axis_index("gz")
    x_hi, x_lo, core = lax.rem(gx, 2), gy // 2, lax.rem(gy, 2)

    def xor(a, b):
        return a + b - 2 * a * b

    def slab_of(b):
        return 2 * xor(b // 2, x_hi) + lax.rem(b, 2)

    def same_slab(a):
        return 2 * xor(slab // 2, lax.rem(a, 2)) + core

    slab = slab_of(gy)
    me = gz * NY + slab

    def dev(a, b, c):
        return {"gx": a, "gy": b, "gz": c}

    def plane_peer(d):
        to = lax.rem(gx + d, NX)
        return dev(to, same_slab(to), gz)

    def remote(s, d, stage, k, where):
        pltpu.make_async_remote_copy(
            src_ref=s, dst_ref=d, send_sem=send.at[stage], recv_sem=recv.at[stage, k],
            device_id=where, device_id_type=MESH,
        ).start()

    def arrived(ref, sem, name="end"):
        with jax.named_scope(f"w_{name}"):
            pltpu.make_async_copy(ref, ref, sem).wait()

    barrier = pltpu.get_barrier_semaphore()
    for d in range(1, NX):
        pl.semaphore_signal(barrier, inc=1, device_id=plane_peer(d), device_id_type=MESH)
    for c in range(NZ):
        for b in range(NY):
            if b or c:
                pl.semaphore_signal(
                    barrier, inc=1, device_id=dev(gx, lax.rem(gy + b, NY), lax.rem(gz + c, NZ)), device_id_type=MESH
                )

    stage_in = pltpu.make_async_copy(src, staged, ssem)
    stage_in.start()
    my_columns = pl.ds(pl.multiple_of(128 * gy, 128), 128)
    for k, (p, n) in enumerate(FORWARD):
        for j in range(p, p + n):
            pltpu.make_async_copy(
                src.at[pl.ds(16 * slab + 2 * j, 2)], xin.at[j, :, :, my_columns], recv.at[0, k]
            ).start()
    loads = [pltpu.make_async_copy(w, weights.at[i], wsem.at[i]) for i, w in enumerate((fx, fy, fz, iz, iy, ix))]
    for c in loads:
        c.start()
    vloads = [pltpu.make_async_copy(v, s, vsem.at[i]) for i, (v, s) in enumerate(((vx, vxs), (vy, vys), (vz, vzs)))]
    for c in vloads:
        c.start()

    with jax.named_scope("w_barrier"):
        pl.semaphore_wait(barrier, NX - 1 + NZ * NY - 1)
    stage_in.wait()

    for k, (p, n) in enumerate(FORWARD):
        for to in (2 * (1 - x_lo), 2 * (1 - x_lo) + 1, 2 * x_lo + 1 - core):
            for j in range(p, p + n):
                remote(
                    staged.at[pl.ds(16 * slab_of(to) + 2 * j, 2)],
                    xin.at[j, :, :, my_columns],
                    0, k, dev(gx, to, gz),
                )

    lane = lax.broadcasted_iota(jnp.int32, (8, 128), 1)
    sub = lax.broadcasted_iota(jnp.int32, (8, 128), 0)
    low = lane < 64

    def exchange_halves(a, b):
        keep = jnp.broadcast_to(lax.broadcasted_iota(jnp.int32, (1, 128), 1) < 64, a.shape)
        return (
            jnp.where(keep, a, pltpu.roll(b, 64, 1)),
            jnp.where(keep, pltpu.roll(a, 64, 1), b),
        )

    for c in vloads:
        c.wait()
    along_p = jnp.zeros((8, 128), F32)
    for i in range(64):
        along_p = jnp.where((lane & 63) == i, vxs[64 * gx + i], along_p)
    along_qp = [
        along_p + jnp.where(low, vys[16 * me + q], vys[16 * me + q + 8]) for q in range(8)
    ]

    def reciprocals(g, _):
        col = jnp.zeros((8, 128), F32)
        for i in range(8):
            col = jnp.where(sub == i, vzs[8 * g + i], col)
        rows = pl.ds(pl.multiple_of(8 * g, 8), 8)
        for q in range(8):
            recip[rows, 128 * q : 128 * (q + 1)] = 1.0 / (col + along_qp[q])
        return 0

    lax.fori_loop(0, N // 8, reciprocals, 0)

    loads[3].wait()
    row = lax.broadcasted_iota(jnp.int32, (N, N), 0)
    wanted = ((row & 63) >> 1) * 16 + (row >> 6) * 2 + (row & 1)
    order = (lax.broadcasted_iota(jnp.int32, (N, N), 1) == wanted).astype(F32).astype(BF16)
    izp[...] = dot(order, weights[3]).astype(BF16)

    my_block = pl.ds(pl.multiple_of(64 * gx, 64), 64)
    my_lines = pl.ds(pl.multiple_of(16 * me, 16), 16)

    def forward_x(k):
        p, n = FORWARD[k]
        arrived(xin.at[p : p + n], recv.at[0, k], f"x{k}")
        o = dot_t(xin[p : p + n].reshape(128 * n, N), weights[0]).reshape(n, 2, 64, N)
        for j in range(n):
            for t in range(4):
                a, b = exchange_halves(o[j, 0, :, 128 * t : 128 * (t + 1)], o[j, 1, :, 128 * t : 128 * (t + 1)])
                psend[2 * t, p + j] = a.astype(BF16)
                psend[2 * t + 1, p + j] = b.astype(BF16)
        for d in range(1, NX):
            to = lax.rem(gx + d, NX)
            remote(psend.at[to, p : p + n], ybuf.at[p : p + n, my_block, :], 1, k, plane_peer(d))
        for j in range(p, p + n):
            ybuf[j, my_block, :] = psend[gx, j]

    to_gz = [lax.rem(gz + c, NZ) for c in range(NZ)]
    near = [[2 * x_lo + c, 2 * (1 - x_lo) + c] for c in range(2)]
    near_slab = [[slab_of(b) for b in pair] for pair in near]
    partner = 2 * x_lo + 1 - core

    def line_peers(half):
        for c in FAR_FIRST:
            for b, place in zip(near[half], near_slab[half]):
                yield to_gz[c] * NY + place, dev(gx, b, to_gz[c])
        yield gz * NY + near_slab[half][1], dev(gx, near[half][1], gz)
        if half == 0:
            yield gz * NY + slab_of(partner), dev(gx, partner, gz)

    def forward_y(k):
        p, n = FORWARD[k]
        arrived(psend.at[0 : NX - 1, p : p + n], recv.at[1, k], f"y{k}")
        o = dot(weights[1], jnp.concatenate([ybuf[j] for j in range(p, p + n)], axis=1))
        for j in range(n):
            yout[p + j] = o[:, 128 * j : 128 * (j + 1)].astype(BF16)

        for j in range(p, p + n):
            zbuf[me, j] = yout[j, my_lines, :]

    def send_lines(k, half):
        p, n = FORWARD[k]
        for place, where in line_peers(half):
            rows = pl.ds(pl.multiple_of(16 * place, 16), 16)
            remote(yout.at[p : p + n, rows, :], zbuf.at[me, p : p + n], 2, k, where)

    def to_z_rows(k):
        p, n = FORWARD[k]
        arrived(zbuf.at[0 : NZ * NY - 1, p : p + n], recv.at[2, k], f"z{k}")

        def some(g, _):
            for s in range(8):
                for j in range(p, p + n):
                    tile = zbuf[8 * g + s, j].astype(F32)
                    a, b = exchange_halves(tile[:8], tile[8:])
                    z = 16 * (8 * g + s) + 2 * j
                    zlines[pl.ds(z, 8, stride=PITCH), :] = a
                    zlines[pl.ds(z + 1, 8, stride=PITCH), :] = b
            return 0

        lax.fori_loop(0, 4, some, 0)

    def along_z():
        for h in range(4):
            d = jnp.concatenate(
                [zlines[PITCH * q : PITCH * q + N, :] for q in (2 * h, 2 * h + 1)], axis=1
            ).astype(BF16)
            c = dot(weights[2], d).astype(BF16).astype(F32)
            scaled[:, 256 * h : 256 * (h + 1)] = (c * recip[:, 256 * h : 256 * (h + 1)]).astype(BF16)

    def from_z_rows(k):
        p, n = INVERSE[k]
        for h in range(4):
            o = dot(izp[64 * p : 64 * (p + n), :], scaled[:, 256 * h : 256 * (h + 1)])
            for j in range(2):
                at = PITCH * (2 * h + j) + 64 * p
                olines[at : at + 64 * n, :] = o[:, 128 * j : 128 * (j + 1)]

        def some(g, _):
            for s in range(8):
                for j in range(p, p + n):
                    at = 64 * j + 2 * (8 * g + s)
                    a, b = exchange_halves(
                        olines[pl.ds(at, 8, stride=PITCH), :], olines[pl.ds(at + 1, 8, stride=PITCH), :]
                    )
                    zsend[8 * g + s, j] = jnp.concatenate([a, b], axis=0).astype(BF16)
            return 0

        lax.fori_loop(0, 4, some, 0)

        for half in range(2):
            for place, where in line_peers(half):
                remote(zsend.at[place, p : p + n], ybuf2.at[p : p + n, my_lines, :], 3, k, where)
        for j in range(p, p + n):
            ybuf2[j, my_lines, :] = zsend[me, j]

    def inverse_y(k):
        p, n = INVERSE[k]
        arrived(zsend.at[0 : NZ * NY - 1, p : p + n], recv.at[3, k], f"yi{k}")
        o = dot(weights[4], jnp.concatenate([ybuf2[j] for j in range(p, p + n)], axis=1))
        for j in range(n):
            yout2[p + j] = o[:, 128 * j : 128 * (j + 1)].astype(BF16)
        for d in range(1, NX):
            to = lax.rem(gx + d, NX)
            rows = pl.ds(pl.multiple_of(64 * to, 64), 64)
            remote(yout2.at[p : p + n, rows, :], pbuf.at[gx, p : p + n], 4, k, plane_peer(d))
        for j in range(p, p + n):
            pbuf[gx, j] = yout2[j, my_block, :]

    def inverse_x(k):
        p, n = INVERSE[k]
        arrived(pbuf.at[0 : NX - 1, p : p + n], recv.at[4, k], f"xi{k}")
        for j in range(p, p + n):
            for t in range(4):
                a, b = exchange_halves(pbuf[2 * t, j].astype(F32), pbuf[2 * t + 1, j].astype(F32))
                xg[2 * j, :, 128 * t : 128 * (t + 1)] = a.astype(BF16)
                xg[2 * j + 1, :, 128 * t : 128 * (t + 1)] = b.astype(BF16)
        here = slice(2 * p, 2 * (p + n))
        o = dot_t(xg[here].reshape(128 * n, N), weights[5])
        xout[here] = o.astype(BF16).reshape(2 * n, 64, N)
        mine = pl.ds(16 * slab + 2 * p, 2 * n)
        for d in (2, 3, 1):
            to = lax.rem(gy + d, NY)
            columns = pl.ds(pl.multiple_of(128 * to, 128), 128)
            remote(xout.at[here, :, columns], out.at[mine], 5, 0, dev(gx, to, gz))
        out[mine] = xout[here, :, my_columns]

    loads[0].wait()
    loads[1].wait()
    for stage, *k in FORWARD_ORDER:
        {"x": forward_x, "y": forward_y, "z": send_lines}[stage](*k)
    for k in range(len(FORWARD)):
        to_z_rows(k)
    loads[2].wait()
    with jax.named_scope("c_z"):
        along_z()
    for k in range(len(INVERSE)):
        with jax.named_scope(f"c_from{k}"):
            from_z_rows(k)
    loads[4].wait()
    loads[5].wait()
    for stage, k in INVERSE_ORDER:
        (inverse_x if stage == "x" else inverse_y)(k)

    arrived(staged.at[0:48], recv.at[5, 0])
    arrived(staged.at[0:48], send.at[0])
    arrived(staged.at[0:48], send.at[5])
    arrived(psend.at[0 : NX - 1], send.at[1])
    arrived(psend.at[0 : NX - 1], send.at[4])
    arrived(zbuf.at[0 : NZ * NY - 1], send.at[2])
    arrived(zbuf.at[0 : NZ * NY - 1], send.at[3])


def on_device(source, *rest):
    pieces = pltpu.VMEM((NX, PAIRS, 64, 128), BF16)
    planes = pltpu.VMEM((PAIRS, N, 128), BF16)
    lines = pltpu.VMEM((NZ * NY, PAIRS, 16, 128), BF16)
    pencils = pltpu.VMEM((2 * PAIRS, 64, N), BF16)
    stages = max(len(FORWARD), len(INVERSE))
    return pl.pallas_call(
        kernel,
        out_shape=pltpu.VMEM(source.shape, BF16),
        in_specs=[pl.BlockSpec(memory_space=pl.ANY)] * 10,
        out_specs=pl.BlockSpec(memory_space=pltpu.VMEM),
        scratch_shapes=[
            pltpu.VMEM(source.shape, BF16),
            pltpu.VMEM((PAIRS, 2, 64, N), BF16),
            pieces,
            planes,
            planes,
            lines,
            pltpu.VMEM((8 * PITCH, 128), F32),
            pltpu.VMEM((N, 1024), F32),
            pltpu.VMEM((N, 1024), BF16),
            pltpu.VMEM((8 * PITCH, 128), F32),
            lines,
            planes,
            planes,
            pieces,
            pencils,
            pencils,
            pltpu.VMEM((6, N, N), BF16),
            pltpu.VMEM((N, N), BF16),
            pltpu.SMEM((N,), F32),
            pltpu.SMEM((N,), F32),
            pltpu.SMEM((N,), F32),
            pltpu.SemaphoreType.DMA((6, stages)),
            pltpu.SemaphoreType.DMA((6,)),
            pltpu.SemaphoreType.DMA((6,)),
            pltpu.SemaphoreType.DMA((3,)),
            pltpu.SemaphoreType.DMA,
        ],
        compiler_params=pltpu.CompilerParams(
            collective_id=0, has_side_effects=True, vmem_limit_bytes=60 * 1024 * 1024
        ),
    )(source, *rest)


def solution(mesh):
    return jax.shard_map(
        on_device,
        mesh=mesh,
        in_specs=(P("gz", "gx", "gy"),) + (P(),) * 9,
        out_specs=P("gz", "gx", "gy"),
        check_vma=False,
    )
```

time: 98.8 us -> 80 us (0.81)
  Pallas kernels: 96.4 us -> 78.8 us
  local copies, waits for them, and re-layouts: 2.26 us -> 0.97 us
    pallas_call x1, Pallas kernels: 96.4 us -> 78.8 us  [on_device(): pl.pallas_call(kernel, out_shape=pltpu.VMEM(source.shape, BF16), in_specs...]
    unnamed x1, local copies, waits for them, and re-layouts: 2.26 us -> 0.97 us
where the time goes in v2:
time: 80 us; the launch traced here: 79.8 us
  Pallas kernels  78.8 us (98%)
  local copies, waits for them, and re-layouts  0.97 us (1%)
    pallas_call x1, Pallas kernels, on_device(): pl.pallas_call(kernel, out_shape=pltpu.VMEM(source.shape, BF16), in_specs...  78.8 us

profile of v2, /device:TPU:1, one launch (start us, length us, event | category | flops | bytes accessed | tf_op | source)
XLA Modules:
  0.0 79.8 jit_solution(1257778331756096906)
XLA Ops:
  0.0 78.8 %shard_map.100 = bf16[64,64,128]{2,1,0:T(8,128)(2,1)S(1)} custom-call(bf16[64,64,128]{2,1,0:T(8,128)(2,1)} %src.1, bf16[512,512]{1,0:T(8,128)(2,1)} %fx.1, bf16[512,512]{1,0:T(8,128)(2,1)} %fy.1, bf16[512,512]{1,0:T(8,128)(2,1)} %fz.1, bf16[512,512]{1,0:T(8,128)(2,1)} %ix.1, bf16[512,512]{1,0:T(8,128)(2,1)} %iy.1, bf16[512,512]{1,0:T(8,128)(2,1)} %iz.1, ...), custom_call_target="tpu_custom_call" | custom-call | tf_op jit(solution)/shard_map/pallas_call | solution.py:306
  78.8 1.0 %copy.12 = bf16[64,64,128]{2,1,0:T(8,128)(2,1)} copy(bf16[64,64,128]{2,1,0:T(8,128)(2,1)S(1)} %shard_map.100) | data formatting | bytes 2097152

commit v3 on v2

--- a/solution.py
+++ b/solution.py
@@ -18,9 +18,12 @@
     ("x", 3), ("y", 2), ("z", 2, 0), ("z", 2, 1), ("x", 4), ("y", 3), ("z", 3, 0), ("y", 4), ("z", 4, 0),
     ("z", 3, 1), ("z", 4, 1),
 )
-INVERSE_ORDER = (("y", 0), ("y", 1), ("x", 0), ("y", 2), ("x", 1), ("y", 3), ("x", 2), ("y", 4), ("x", 3), ("y", 5), ("x", 4), ("x", 5))
+INVERSE_ORDER = (
+    ("y", 0), ("y", 1), ("x", 0), ("y", 2), ("x", 1), ("y", 3), ("y", 4), ("x", 2), ("y", 5), ("x", 3), ("x", 4), ("x", 5),
+)
 PITCH = N + 8
 FAR_FIRST = (4, 3, 5, 2, 6, 1, 7)
+PLANE_FAR_FIRST = ((2, 1), (1, 1), (3, 1), (2, 0), (0, 1), (1, 0), (3, 0))
 
 
 def dot(a, b):
@@ -34,7 +37,7 @@
 def kernel(
     src, fx, fy, fz, ix, iy, iz, vx, vy, vz, out,
     staged, xin, psend, ybuf, yout, zbuf, zlines, recip, scaled, olines, zsend, ybuf2, yout2, pbuf, xg, xout,
-    weights, izp, vxs, vys, vzs, recv, send, wsem, vsem, ssem,
+    weights, izp, vxs, vys, vzs, recv, send, wsem, vsem, ssem, ready,
 ):
     gx, gy, gz = lax.axis_index("gx"), lax.axis_index("gy"), lax.axis_index("gz")
     x_hi, x_lo, core = lax.rem(gx, 2), gy // 2, lax.rem(gy, 2)
@@ -54,9 +57,10 @@
     def dev(a, b, c):
         return {"gx": a, "gy": b, "gz": c}
 
-    def plane_peer(d):
-        to = lax.rem(gx + d, NX)
-        return dev(to, same_slab(to), gz)
+    plane_peers = []
+    for d, h in PLANE_FAR_FIRST:
+        to = 2 * lax.rem(gx // 2 + d, NX // 2) + (xor(x_hi, 1) if h else x_hi)
+        plane_peers.append((to, dev(to, same_slab(to), gz)))
 
     def remote(s, d, stage, k, where):
         pltpu.make_async_remote_copy(
@@ -69,14 +73,15 @@
             pltpu.make_async_copy(ref, ref, sem).wait()
 
     barrier = pltpu.get_barrier_semaphore()
-    for d in range(1, NX):
-        pl.semaphore_signal(barrier, inc=1, device_id=plane_peer(d), device_id_type=MESH)
-    for c in range(NZ):
-        for b in range(NY):
-            if b or c:
-                pl.semaphore_signal(
-                    barrier, inc=1, device_id=dev(gx, lax.rem(gy + b, NY), lax.rem(gz + c, NZ)), device_id_type=MESH
-                )
+    for _, where in plane_peers:
+        pl.semaphore_signal(barrier, inc=1, device_id=where, device_id_type=MESH)
+    for b in range(1, NY):
+        pl.semaphore_signal(barrier, inc=1, device_id=dev(gx, lax.rem(gy + b, NY), gz), device_id_type=MESH)
+    for c in range(1, NZ):
+        @pl.when(c > gz)
+        def _():
+            for b in range(NY):
+                pl.semaphore_signal(barrier, inc=1, device_id=dev(gx, b, c), device_id_type=MESH)
 
     stage_in = pltpu.make_async_copy(src, staged, ssem)
     stage_in.start()
@@ -94,7 +99,7 @@
         c.start()
 
     with jax.named_scope("w_barrier"):
-        pl.semaphore_wait(barrier, NX - 1 + NZ * NY - 1)
+        pl.semaphore_wait(barrier, NX - 1 + NY - 1 + NY * gz)
     stage_in.wait()
 
     for k, (p, n) in enumerate(FORWARD):
@@ -105,6 +110,12 @@
                     xin.at[j, :, :, my_columns],
                     0, k, dev(gx, to, gz),
                 )
+
+    for c in range(NZ - 1):
+        @pl.when(c < gz)
+        def _():
+            for b in range(NY):
+                pl.semaphore_signal(ready, inc=1, device_id=dev(gx, b, c), device_id_type=MESH)
 
     lane = lax.broadcasted_iota(jnp.int32, (8, 128), 1)
     sub = lax.broadcasted_iota(jnp.int32, (8, 128), 0)
@@ -155,9 +166,8 @@
                 a, b = exchange_halves(o[j, 0, :, 128 * t : 128 * (t + 1)], o[j, 1, :, 128 * t : 128 * (t + 1)])
                 psend[2 * t, p + j] = a.astype(BF16)
                 psend[2 * t + 1, p + j] = b.astype(BF16)
-        for d in range(1, NX):
-            to = lax.rem(gx + d, NX)
-            remote(psend.at[to, p : p + n], ybuf.at[p : p + n, my_block, :], 1, k, plane_peer(d))
+        for to, where in plane_peers:
+            remote(psend.at[to, p : p + n], ybuf.at[p : p + n, my_block, :], 1, k, where)
         for j in range(p, p + n):
             ybuf[j, my_block, :] = psend[gx, j]
 
@@ -186,6 +196,11 @@
 
     def send_lines(k, half):
         p, n = FORWARD[k]
+        if (k, half) == (0, 0):
+            @pl.when(gz < NZ - 1)
+            def _():
+                pl.semaphore_wait(ready, NY * (NZ - 1 - gz))
+
         for place, where in line_peers(half):
             rows = pl.ds(pl.multiple_of(16 * place, 16), 16)
             remote(yout.at[p : p + n, rows, :], zbuf.at[me, p : p + n], 2, k, where)
@@ -246,10 +261,9 @@
         o = dot(weights[4], jnp.concatenate([ybuf2[j] for j in range(p, p + n)], axis=1))
         for j in range(n):
             yout2[p + j] = o[:, 128 * j : 128 * (j + 1)].astype(BF16)
-        for d in range(1, NX):
-            to = lax.rem(gx + d, NX)
+        for to, where in plane_peers:
             rows = pl.ds(pl.multiple_of(64 * to, 64), 64)
-            remote(yout2.at[p : p + n, rows, :], pbuf.at[gx, p : p + n], 4, k, plane_peer(d))
+            remote(yout2.at[p : p + n, rows, :], pbuf.at[gx, p : p + n], 4, k, where)
         for j in range(p, p + n):
             pbuf[gx, j] = yout2[j, my_block, :]
 
@@ -335,6 +349,7 @@
             pltpu.SemaphoreType.DMA((6,)),
             pltpu.SemaphoreType.DMA((3,)),
             pltpu.SemaphoreType.DMA,
+            pltpu.SemaphoreType.REGULAR,
         ],
         compiler_params=pltpu.CompilerParams(
             collective_id=0, has_side_effects=True, vmem_limit_bytes=60 * 1024 * 1024

time: 80 us -> 77 us (0.963)
  Pallas kernels: 78.8 us -> 75.9 us
    pallas_call x1, Pallas kernels: 78.8 us -> 75.9 us  [on_device(): pl.pallas_call(kernel, out_shape=pltpu.VMEM(source.shape, BF16), in_specs...]
where the time goes in v3:
time: 77 us; the launch traced here: 76.9 us
  Pallas kernels  75.9 us (99%)
  local copies, waits for them, and re-layouts  0.97 us (1%)
    pallas_call x1, Pallas kernels, on_device(): pl.pallas_call(kernel, out_shape=pltpu.VMEM(source.shape, BF16), in_specs...  75.9 us

profile of v3, /device:TPU:1, one launch (start us, length us, event | category | flops | bytes accessed | tf_op | source)
XLA Modules:
  0.0 76.9 jit_solution(17647485714565183463)
XLA Ops:
  0.0 75.9 %shard_map.100 = bf16[64,64,128]{2,1,0:T(8,128)(2,1)S(1)} custom-call(bf16[64,64,128]{2,1,0:T(8,128)(2,1)} %src.1, bf16[512,512]{1,0:T(8,128)(2,1)} %fx.1, bf16[512,512]{1,0:T(8,128)(2,1)} %fy.1, bf16[512,512]{1,0:T(8,128)(2,1)} %fz.1, bf16[512,512]{1,0:T(8,128)(2,1)} %ix.1, bf16[512,512]{1,0:T(8,128)(2,1)} %iy.1, bf16[512,512]{1,0:T(8,128)(2,1)} %iz.1, ...), custom_call_target="tpu_custom_call" | custom-call | tf_op jit(solution)/shard_map/pallas_call | solution.py:320
  75.9 1.0 %copy.12 = bf16[64,64,128]{2,1,0:T(8,128)(2,1)} copy(bf16[64,64,128]{2,1,0:T(8,128)(2,1)S(1)} %shard_map.100) | data formatting | bytes 2097152

commit v4 on v3

--- a/solution.py
+++ b/solution.py
@@ -10,6 +10,7 @@
 BF16 = jnp.bfloat16
 NX, NY, NZ = 8, 4, 8
 N = 512
+EARLY = 2
 PAIRS = 8
 FORWARD = ((0, 1), (1, 1), (2, 2), (4, 2), (6, 2))
 INVERSE = ((0, 1), (1, 2), (3, 2), (5, 1), (6, 1), (7, 1))
@@ -78,7 +79,7 @@
     for b in range(1, NY):
         pl.semaphore_signal(barrier, inc=1, device_id=dev(gx, lax.rem(gy + b, NY), gz), device_id_type=MESH)
     for c in range(1, NZ):
-        @pl.when(c > gz)
+        @pl.when((gz < c) & (gz < EARLY))
         def _():
             for b in range(NY):
                 pl.semaphore_signal(barrier, inc=1, device_id=dev(gx, b, c), device_id_type=MESH)
@@ -99,7 +100,7 @@
         c.start()
 
     with jax.named_scope("w_barrier"):
-        pl.semaphore_wait(barrier, NX - 1 + NY - 1 + NY * gz)
+        pl.semaphore_wait(barrier, NX - 1 + NY - 1 + NY * jnp.minimum(gz, EARLY))
     stage_in.wait()
 
     for k, (p, n) in enumerate(FORWARD):
@@ -111,7 +112,7 @@
                     0, k, dev(gx, to, gz),
                 )
 
-    for c in range(NZ - 1):
+    for c in range(EARLY):
         @pl.when(c < gz)
         def _():
             for b in range(NY):
@@ -197,9 +198,18 @@
     def send_lines(k, half):
         p, n = FORWARD[k]
         if (k, half) == (0, 0):
-            @pl.when(gz < NZ - 1)
+            @pl.when(gz < EARLY)
             def _():
                 pl.semaphore_wait(ready, NY * (NZ - 1 - gz))
+
+            @pl.when(gz >= EARLY)
+            def _():
+                pl.semaphore_wait(ready, 1)
+
+            @pl.when(gz == 0)
+            def _():
+                for c in range(EARLY, NZ):
+                    pl.semaphore_signal(ready, inc=1, device_id=dev(gx, gy, c), device_id_type=MESH)
 
         for place, where in line_peers(half):
             rows = pl.ds(pl.multiple_of(16 * place, 16), 16)
@@ -329,10 +339,10 @@
             planes,
             planes,
             lines,
-            pltpu.VMEM((8 * PITCH, 128), F32),
+            pltpu.VMEM((9 * PITCH, 128), F32),
             pltpu.VMEM((N, 1024), F32),
             pltpu.VMEM((N, 1024), BF16),
-            pltpu.VMEM((8 * PITCH, 128), F32),
+            pltpu.VMEM((9 * PITCH, 128), F32),
             lines,
             planes,
             planes,

time: 77 us -> 77 us (level)
  no operation moved by 1% of the time
where the time goes in v4:
time: 77 us
  Pallas kernels  76 us (99%)
  local copies, waits for them, and re-layouts  0.97 us (1%)
    pallas_call x1, Pallas kernels, on_device(): pl.pallas_call(kernel, out_shape=pltpu.VMEM(source.shape, BF16), in_specs...  76 us

profile of v4, /device:TPU:1, one launch (start us, length us, event | category | flops | bytes accessed | tf_op | source)
XLA Modules:
  0.0 77.0 jit_solution(15803271850956770974)
XLA Ops:
  0.0 76.0 %shard_map.100 = bf16[64,64,128]{2,1,0:T(8,128)(2,1)S(1)} custom-call(bf16[64,64,128]{2,1,0:T(8,128)(2,1)} %src.1, bf16[512,512]{1,0:T(8,128)(2,1)} %fx.1, bf16[512,512]{1,0:T(8,128)(2,1)} %fy.1, bf16[512,512]{1,0:T(8,128)(2,1)} %fz.1, bf16[512,512]{1,0:T(8,128)(2,1)} %ix.1, bf16[512,512]{1,0:T(8,128)(2,1)} %iy.1, bf16[512,512]{1,0:T(8,128)(2,1)} %iz.1, ...), custom_call_target="tpu_custom_call" | custom-call | tf_op jit(solution)/shard_map/pallas_call | solution.py:330
  76.0 1.0 %copy.12 = bf16[64,64,128]{2,1,0:T(8,128)(2,1)} copy(bf16[64,64,128]{2,1,0:T(8,128)(2,1)S(1)} %shard_map.100) | data formatting | bytes 2097152

commit v5 on v3

--- a/solution.py
+++ b/solution.py
@@ -279,8 +279,7 @@
         o = dot_t(xg[here].reshape(128 * n, N), weights[5])
         xout[here] = o.astype(BF16).reshape(2 * n, 64, N)
         mine = pl.ds(16 * slab + 2 * p, 2 * n)
-        for d in (2, 3, 1):
-            to = lax.rem(gy + d, NY)
+        for to in (2 * (1 - x_lo), 2 * (1 - x_lo) + 1, 2 * x_lo + 1 - core):
             columns = pl.ds(pl.multiple_of(128 * to, 128), 128)
             remote(xout.at[here, :, columns], out.at[mine], 5, 0, dev(gx, to, gz))
         out[mine] = xout[here, :, my_columns]

time: 77 us -> 77 us (level)
  no operation moved by 1% of the time
where the time goes in v5:
time: 77 us; the launch traced here: 76.9 us
  Pallas kernels  75.9 us (99%)
  local copies, waits for them, and re-layouts  0.97 us (1%)
    pallas_call x1, Pallas kernels, on_device(): pl.pallas_call(kernel, out_shape=pltpu.VMEM(source.shape, BF16), in_specs...  75.9 us

profile of v5, /device:TPU:1, one launch (start us, length us, event | category | flops | bytes accessed | tf_op | source)
XLA Modules:
  0.0 76.9 jit_solution(6397128143470713758)
XLA Ops:
  0.0 75.9 %shard_map.100 = bf16[64,64,128]{2,1,0:T(8,128)(2,1)S(1)} custom-call(bf16[64,64,128]{2,1,0:T(8,128)(2,1)} %src.1, bf16[512,512]{1,0:T(8,128)(2,1)} %fx.1, bf16[512,512]{1,0:T(8,128)(2,1)} %fy.1, bf16[512,512]{1,0:T(8,128)(2,1)} %fz.1, bf16[512,512]{1,0:T(8,128)(2,1)} %ix.1, bf16[512,512]{1,0:T(8,128)(2,1)} %iy.1, bf16[512,512]{1,0:T(8,128)(2,1)} %iz.1, ...), custom_call_target="tpu_custom_call" | custom-call | tf_op jit(solution)/shard_map/pallas_call | solution.py:319
  75.9 1.0 %copy.12 = bf16[64,64,128]{2,1,0:T(8,128)(2,1)} copy(bf16[64,64,128]{2,1,0:T(8,128)(2,1)S(1)} %shard_map.100) | data formatting | bytes 2097152
